TPU v7x, 32 devices: a whole 2x2x4 slice. The times are simulated.
32 devices in a mesh: section: 4 (over x, core), dp: 8 (over z, y).
Axes of the slice: x: 2, y: 2, z: 4, core: 2. Of those that a mesh axis runs over, the one named last changes fastest.
Arguments:
- student_states: bfloat16 [64, 512, 1024], P('dp'), may hold values from -6 to 6
- lengths: int32 [64], P('dp'), may hold values from 64 to 512
- student_ln_gain: float32 [1024], replicated, may hold values from 0.1 to 1.9
- student_w_in: bfloat16 [1024, 4096], P(None, 'section'), may hold values from -0.1875 to 0.1875
- student_w_out: bfloat16 [4096, 1024], P('section'), may hold values from -0.09375 to 0.09375
- teacher_rows: bfloat16 [64, 4096], P('dp'), may hold values from -6 to 6
- teacher_mlp_gain: float32 [4096], replicated, may hold values from 0.1 to 1.9
- teacher_gate_up: bfloat16 [2, 4096, 12288], P(None, 'dp', 'section'), may hold values from -0.09375 to 0.09375
- teacher_down: bfloat16 [12288, 4096], P('section', 'dp'), may hold values from -0.0546875 to 0.0546875
- teacher_final_gain: float32 [4096], replicated, may hold values from 0.1 to 1.9
Outputs:
- loss: float32 [], replicated
- grad_w_in: float32 [1024, 4096], P('dp', 'section')
- grad_w_out: float32 [4096, 1024], P(('section', 'dp'))
- teacher_states: float32 [64, 4096], P('dp', 'section')
Inputs may be any that keep to these rules, and one draw needn't show every extreme that they name: Each document's first lengths tokens are real, the rest padding.
All inputs are finite; a program needn't handle non-finite values.
Results may differ from a plain program's by a relative error of at most 0.013.
The roundings to bfloat16 on the way count: a program that leaves them out, or rounds other values in their place, can miss the bound.
Values may be sent and summed in bfloat16 or wider, within the bound.
No kernel may reach another device: no remote copies, remote signals or barrier semaphores. Data moves between devices by JAX's collectives and lax.ppermute only.
A program may use at most 128 MiB of HBM per device.

v0:
```python
import jax
import jax.numpy as jnp
from jax import lax
from jax.sharding import PartitionSpec as P

student_softness = 0.05
teacher_softness = 0.02


def layer_norm(states, gain):
    values = states.astype(jnp.float32)
    center = values - jnp.mean(values, -1, keepdims=True)
    spread = jnp.mean(center * center, -1, keepdims=True)
    return (center * lax.rsqrt(spread + 1e-05) * gain).astype(jnp.bfloat16)


def gelu_exact(value):
    return 0.5 * value * (1.0 + jax.scipy.special.erf(value * 0.7071067811865476))


def gelu_slope(value):
    return (
        0.5 * (1.0 + jax.scipy.special.erf(value * 0.7071067811865476))
        + value * jnp.exp(-0.5 * value * value) * 0.3989422804014327
    )


def contrast(student_logits, teacher_logits, row_ids, col_ids):
    keep = row_ids[:, None] != col_ids[None, :]
    partner = (row_ids + 1 - 2 * (row_ids % 2))[:, None] == col_ids[None, :]
    s_exp = jnp.where(keep, jnp.exp(student_logits), 0.0)
    t_exp = jnp.where(keep, jnp.exp(teacher_logits), 0.0)
    s_total = jnp.sum(s_exp, -1, keepdims=True)
    t_total = jnp.sum(t_exp, -1, keepdims=True)
    s_prob = s_exp / s_total
    t_prob = t_exp / t_total
    s_log = student_logits - jnp.log(s_total)
    t_log = teacher_logits - jnp.log(t_total)
    terms = jnp.where(partner, -s_log, 0.0) + jnp.where(keep, t_prob * (t_log - s_log), 0.0)
    gradient_list = 2.0 * s_prob - partner.astype(jnp.float32) - t_prob
    return (gradient_list, jnp.sum(terms))


def on_device(
    student_states,
    lengths,
    student_ln_gain,
    student_w_in,
    student_w_out,
    teacher_rows,
    teacher_mlp_gain,
    teacher_gate_up,
    teacher_down,
    teacher_final_gain,
):
    dp_count = lax.axis_size("dp")
    dp_index = lax.axis_index("dp")
    section_index = lax.axis_index("section")
    local_docs = teacher_rows.shape[0]
    total_docs = local_docs * dp_count
    highest_precision = lax.Precision.HIGHEST
    rows_f = teacher_rows.astype(jnp.float32)
    inverse = lax.rsqrt(jnp.mean(rows_f * rows_f, -1, keepdims=True) + 1e-06)
    normed = (rows_f * inverse * teacher_mlp_gain).astype(jnp.bfloat16)
    col_width = teacher_gate_up.shape[1]
    hidden_width = teacher_gate_up.shape[2]
    every_row = lax.all_gather(normed, "dp", axis=0, tiled=True)
    columns = lax.dynamic_slice_in_dim(every_row, dp_index * col_width, col_width, 1)
    gate_part = jnp.dot(columns, teacher_gate_up[0], preferred_element_type=jnp.float32)
    upper_part = jnp.dot(columns, teacher_gate_up[1], preferred_element_type=jnp.float32)
    both = lax.psum_scatter(
        jnp.concatenate([gate_part, upper_part], axis=1), "dp", scatter_dimension=0, tiled=True
    )
    hidden = (jax.nn.silu(both[:, :hidden_width]) * both[:, hidden_width:]).astype(jnp.bfloat16)
    partial_out = jnp.dot(
        lax.all_gather(hidden, "dp", axis=0, tiled=True),
        teacher_down,
        preferred_element_type=jnp.float32,
    )
    per_doc = lax.all_to_all(partial_out, "dp", split_axis=0, concat_axis=1, tiled=True)
    mlp_part = lax.psum_scatter(per_doc, "section", scatter_dimension=1, tiled=True)
    part_width = mlp_part.shape[1]
    teacher_states = (
        lax.dynamic_slice_in_dim(rows_f, section_index * part_width, part_width, 1) + mlp_part
    )
    final_gain = lax.dynamic_slice_in_dim(
        teacher_final_gain, section_index * part_width, part_width, 0
    )
    scaled = teacher_states * final_gain
    teacher_square = jnp.sum(scaled * scaled, -1)
    seq_len = student_states.shape[1]
    width = student_states.shape[2]
    tokens = layer_norm(student_states, student_ln_gain).reshape(local_docs * seq_len, width)
    pre_act = jnp.dot(tokens, student_w_in, preferred_element_type=jnp.float32)
    act = gelu_exact(pre_act).astype(jnp.bfloat16).reshape(local_docs, seq_len, -1)
    positions = jnp.arange(seq_len, dtype=jnp.int32)
    mask_f = (positions[None, :] < lengths[:, None]).astype(jnp.float32)
    mask_low = mask_f.astype(jnp.bfloat16)
    counts = lengths.astype(jnp.float32)[:, None]
    pooled_act = (
        jnp.einsum("bs,bsf->bf", mask_low, act, preferred_element_type=jnp.float32) / counts
    ).astype(jnp.bfloat16)
    pooled_x = (
        jnp.einsum("bs,bse->be", mask_low, student_states, preferred_element_type=jnp.float32)
        / counts
    )
    partial_emb = jnp.dot(pooled_act, student_w_out, preferred_element_type=jnp.float32)
    emb_sum, teacher_total = lax.psum((partial_emb, teacher_square), "section")
    student_raw = pooled_x + emb_sum
    norms = jnp.sqrt(jnp.sum(student_raw * student_raw, -1, keepdims=True) + 1e-06)
    student_normalized = student_raw / norms
    teacher_normalized = scaled / jnp.sqrt(teacher_total[:, None] + 1e-06)
    all_student_rows, every_teacher = (
        lax.all_gather(student_normalized, "dp", axis=0, tiled=True),
        lax.all_gather(teacher_normalized, "dp", axis=0, tiled=True),
    )
    first_row = dp_index * local_docs
    col_ids = jnp.arange(total_docs, dtype=jnp.int32)
    teacher_gram = lax.psum(
        jnp.dot(every_teacher, every_teacher.T, precision=highest_precision), "section"
    )
    teacher_logits = teacher_gram / teacher_softness
    student_logits = (
        jnp.dot(all_student_rows, all_student_rows.T, precision=highest_precision)
        / student_softness
    )
    gradient_list, loss = contrast(student_logits, teacher_logits, col_ids, col_ids)
    symmetric = (
        lax.dynamic_slice_in_dim(gradient_list, first_row, local_docs, 0)
        + lax.dynamic_slice_in_dim(gradient_list, first_row, local_docs, 1).T
    )
    normalized_gradient = (
        jnp.dot(symmetric, all_student_rows, precision=highest_precision) / student_softness
    )
    raw_grad = (
        normalized_gradient
        - student_normalized * jnp.sum(student_normalized * normalized_gradient, -1, keepdims=True)
    ) / norms
    raw_low = raw_grad.astype(jnp.bfloat16)
    grad_out_part = jnp.dot(pooled_act.T, raw_low, preferred_element_type=jnp.float32)
    pool_grad = lax.dot_general(
        raw_low, student_w_out, (((1,), (1,)), ((), ())), preferred_element_type=jnp.float32
    )
    scale = pool_grad / counts
    slope = gelu_slope(pre_act).reshape(local_docs, seq_len, -1)
    act_grad = (
        (slope * mask_f[:, :, None] * scale[:, None, :])
        .astype(jnp.bfloat16)
        .reshape(local_docs * seq_len, -1)
    )
    grad_w_in = lax.psum_scatter(
        lax.dot_general(
            tokens, act_grad, (((0,), (0,)), ((), ())), preferred_element_type=jnp.float32
        ),
        "dp",
        scatter_dimension=0,
        tiled=True,
    )
    grad_w_out = lax.psum_scatter(grad_out_part, "dp", scatter_dimension=0, tiled=True)
    return (loss, grad_w_in, grad_w_out, teacher_states)


def solution(mesh):
    placed = (
        P("dp", None, None),
        P("dp"),
        P(),
        P(None, "section"),
        P("section", None),
        P("dp", None),
        P(),
        P(None, "dp", "section"),
        P("section", "dp"),
        P(),
    )
    return jax.shard_map(
        on_device,
        mesh=mesh,
        in_specs=placed,
        out_specs=(P(), P("dp", "section"), P(("section", "dp"), None), P("dp", "section")),
        check_vma=False,
    )
```

profile of v0, /device:TPU:0, one launch (start us, length us, event | category | flops | bytes accessed | tf_op | source)
XLA Modules:
  0.0 472.4 jit_solution(15966292794362974652)
XLA Ops:
  7.2 0.0 copy-start
  7.2 0.0 reduce-scatter.5.cloned.1.call-start
  7.2 1.1 multiply_reduce_fusion
  8.4 0.9 multiply_convert_fusion.5
  9.3 35.3 %all_gather.13 = bf16[64,4096]{1,0:T(8,128)(2,1)} all-gather(bf16[8,4096]{1,0:T(8,128)(2,1)S(1)} %multiply_convert_fusion.5), channel_id=1, replica_groups=mesh['section'=4,'dp'=8] {'dp'}, dimensions={0}, use_global_device_ids=true | all-gather | bytes 589824 | tf_op jit(solution)/shard_map/all_gather | solution.py:67
  44.6 2.6 fusion.12
  47.2 2.6 fusion.14
  49.8 1.3 pad_maximum_fusion
  51.0 0.0 reduce-scatter.5.cloned.1.call-update
  51.1 0.0 copy-start.7
  51.1 0.0 slice-start
  51.1 0.0 copy-start.6
  51.1 4.7 convert_reduce_fusion
  55.8 0.0 slice-start.1
  55.8 5.7 %fusion.2 = f32[8,512]{1,0:T(8,128)S(1)} fusion(bf16[8,512,1024]{2,1,0:T(8,128)(2,1)} %param.10, f32[8,512]{1,0:T(8,128)S(1)} %broadcast_multiply_fusion), kind=kLoop, calls=%fused_computation.5 | loop fusion | flops 16773120 | bytes 8421376 | tf_op jit(solution)/shard_map/reduce_sum | solution.py:13
  61.6 0.0 copy-done.7
  61.6 0.7 fusion.27
  62.2 0.0 copy-done.6
  62.2 2.8 fusion.4
  65.1 0.0 copy-start.8
  65.1 1.2 fusion.30
  66.3 2.4 copy-done.1
  68.7 0.0 copy-done.8
  68.7 16.7 %fusion.8 = (f32[4096,1024]{1,0:T(8,128)}, bf16[4096,1024]{1,0:T(8,128)(2,1)}) fusion(bf16[4096,1024]{1,0:T(8,128)(2,1)S(1)} %bitcast.56, bf16[1024,1024]{1,0:T(8,128)(2,1)S(1)} %copy-done.8), kind=kOutput, calls=%fused_computation.11 | convolution fusion | flops 8636071936 | bytes 35651584 | tf_op jit(solution)/shard_map/dot_general | solution.py:94
  85.3 32.8 %reduce-scatter.5.cloned.1.call-done = f32[8,6144]{1,0:T(8,128)} async-done(((f32[64,6144]{1,0:T(8,128)}), f32[8,6144]{1,0:T(8,128)}) %reduce-scatter.5.cloned.1.call-update) | async-done | bytes 196624 | tf_op jit(solution)/shard_map/reduce_scatter | solution.py:71
  118.1 1.0 fusion.19
  119.1 31.0 %all_gather.14 = bf16[64,3072]{1,0:T(8,128)(2,1)S(1)} all-gather(bf16[8,3072]{1,0:T(8,128)(2,1)S(1)} %fusion.19), channel_id=1, replica_groups=mesh['section'=4,'dp'=8] {'dp'}, dimensions={0}, use_global_device_ids=true | all-gather | bytes 442368 | tf_op jit(solution)/shard_map/all_gather | solution.py:76
  150.1 1.3 convolution_bitcast_fusion
  151.4 3.4 all-to-all-start
  154.8 0.0 reduce-scatter.7.cloned.1.call-start
  154.9 4.6 fusion.28
  159.4 0.0 copy-done.2
  159.4 0.7 convert_element_type.50
  160.1 0.7 dynamic_slice.17
  160.8 1.3 all-to-all-done
  162.1 0.7 copy-done.3
  162.7 0.0 reduce-scatter.7.cloned.1.call-update
  162.8 0.0 reduce-scatter.9.cloned.1.call-start
  162.8 2.0 fusion.40
  164.8 17.8 %reduce-scatter.7.cloned.1.call-done = f32[8,1024]{1,0:T(8,128)} async-done(((f32[8,4096]{1,0:T(8,128)}), f32[8,1024]{1,0:T(8,128)}) %reduce-scatter.7.cloned.1.call-update) | async-done | bytes 32784 | tf_op jit(solution)/shard_map/reduce_scatter | solution.py:81
  182.6 0.9 multiply_reduce_fusion.2
  183.5 5.8 %psum.22 = f32[8]{0:T(128)S(1)} all-reduce(f32[8]{0:T(128)S(1)} %get-tuple-element.6), channel_id=1, replica_groups=mesh['section'=4,'dp'=8] {'section'}, use_global_device_ids=true, to_apply=%region_9.10 | all-reduce | flops 8 | bytes 64 | tf_op jit(solution)/shard_map/psum | solution.py:108
  189.3 0.1 multiply_divide_fusion
  189.3 31.1 %all_gather.15 = f32[64,1024]{1,0:T(8,128)S(1)} all-gather(f32[8,1024]{1,0:T(8,128)S(1)} %multiply_divide_fusion), channel_id=1, replica_groups=mesh['section'=4,'dp'=8] {'dp'}, dimensions={0}, use_global_device_ids=true | all-gather | bytes 294912 | tf_op jit(solution)/shard_map/all_gather | solution.py:115
  220.5 0.4 fusion.42
  220.9 11.1 %all-reduce = (f32[8,1024]{1,0:T(8,128)S(1)}, f32[64,64]{0,1:T(8,128)S(1)}) all-reduce(f32[8,1024]{1,0:T(8,128)S(1)} %fusion.40, f32[64,64]{0,1:T(8,128)S(1)} %fusion.42), channel_id=1, replica_groups=mesh['section'=4,'dp'=8] {'section'}, use_global_device_ids=true, to_apply=%region_2.3 | all-reduce | flops 12288 | bytes 98304 | tf_op jit(solution)/shard_map/psum | solution.py:108
  232.0 0.0 copy-start.5
  232.0 0.2 multiply_reduce_fusion.3
  232.2 0.1 broadcast_divide_fusion
  232.3 30.9 %all_gather.12 = f32[64,1024]{1,0:T(8,128)S(1)} all-gather(f32[8,1024]{1,0:T(8,128)S(1)} %broadcast_divide_fusion), channel_id=1, replica_groups=mesh['section'=4,'dp'=8] {'dp'}, dimensions={0}, use_global_device_ids=true | all-gather | bytes 294912 | tf_op jit(solution)/shard_map/all_gather | solution.py:114
  263.2 0.4 fusion.24
  263.7 1.4 subtract_subtract_fusion
  265.1 0.7 constant_dynamic-slice_fusion
  265.8 0.8 copy.22
  266.6 0.4 multiply_reduce_fusion.1
  266.9 0.1 divide_convert_fusion
  267.0 2.2 convolution_divide_fusion
  269.3 16.3 %fusion.18 = f32[1024,1024]{1,0:T(8,128)} fusion(bf16[8,512,1024]{2,1,0:T(8,128)(2,1)} %copy-done.1, f32[8,512,1024]{2,1,0:T(8,128)} %bitcast.58, f32[8,1024]{1,0:T(8,128)S(1)} %convolution_divide_fusion, f32[8,512]{1,0:T(8,128)} %get-tuple-element.12), kind=kOutput, calls=%fused_computation.24 | convolution fusion | flops 8602517504 | bytes 29409280 | tf_op jit(solution)/shard_map/dot_general | solution.py:152
  285.6 0.0 reduce-scatter.9.cloned.1.call-update
  285.6 0.0 reduce-scatter.11.cloned.1.call-start
  285.6 2.7 fusion.38
  288.4 0.0 reduce-scatter.11.cloned.1.call-update
  288.4 85.4 %reduce-scatter.9.cloned.1.call-done = f32[128,1024]{1,0:T(8,128)} async-done(((f32[1024,1024]{1,0:T(8,128)}), f32[128,1024]{1,0:T(8,128)}) %reduce-scatter.9.cloned.1.call-update) | async-done | bytes 524304 | tf_op jit(solution)/shard_map/reduce_scatter | solution.py:151
  373.8 92.1 %reduce-scatter.11.cloned.1.call-done = f32[128,1024]{1,0:T(8,128)} async-done(((f32[1024,1024]{1,0:T(8,128)}), f32[128,1024]{1,0:T(8,128)}) %reduce-scatter.11.cloned.1.call-update) | async-done | bytes 524304 | tf_op jit(solution)/shard_map/reduce_scatter | solution.py:159
  (20 shorter events, 0.1 us)
Async XLA Ops:
  7.2 142.9 %copy-start = (bf16[3072,512]{1,0:T(8,128)(2,1)S(1)}, bf16[3072,512]{1,0:T(8,128)(2,1)}, u32[]{:S(2)}) copy-start(bf16[3072,512]{1,0:T(8,128)(2,1)} %param.18) | copy-start | bytes 9437188
  7.2 110.9 %reduce-scatter.5.cloned.1.call-start = ((), (), s32[]{:S(2)}) async-start(), calls=%async_computation.5 | async-start | bytes 1769472 | tf_op jit(solution)/shard_map/reduce_scatter | solution.py:71
  51.1 10.5 %copy-start.7 = (s32[8]{0:T(128)S(1)}, s32[8]{0:T(128)}, u32[]{:S(2)}) copy-start(s32[8]{0:T(128)} %param.11) | copy-start | bytes 100
  51.1 11.2 %slice-start = ((s8[8388608]{0:T(1024)(128)(4,1)}), s8[4194304]{0:T(1024)(128)(4,1)S(1)}, s32[]{:S(2)}) async-start(s8[8388608]{0:T(1024)(128)(4,1)} %bitcast.53), calls=%async_computation.9 | async-start | bytes 8388608
  51.1 11.2 %copy-start.6 = (f32[1024]{0:T(1024)S(1)}, f32[1024]{0:T(1024)}, u32[]{:S(2)}) copy-start(f32[1024]{0:T(1024)} %param.12) | copy-start | bytes 12292
  55.8 6.4 %slice-start.1 = ((s8[8388608]{0:T(1024)(128)(4,1)}), s8[4194304]{0:T(1024)(128)(4,1)S(1)}, s32[]{:S(2)}) async-start(s8[8388608]{0:T(1024)(128)(4,1)} %bitcast.53), calls=%async_computation.10 | async-start | bytes 8388608
  65.1 3.6 copy-start.1
  65.1 3.6 copy-start.8
  85.3 74.1 %copy-start.2 = (bf16[8,4096]{1,0:T(8,128)(2,1)S(1)}, bf16[8,4096]{1,0:T(8,128)(2,1)}, u32[]{:S(2)}) copy-start(bf16[8,4096]{1,0:T(8,128)(2,1)} %param.15) | copy-start | bytes 196612
  151.4 10.7 %all-to-all-start = ((f32[8,8,512]{2,1,0:T(8,128)}), f32[8,8,512]{2,1,0:T(8,128)S(1)}, u32[]{:S(2)}, u32[]{:S(2)}) async-start(f32[8,8,512]{2,1,0:T(8,128)} %convolution_bitcast_fusion), calls=%async_computation.1 | async-start | bytes 262144 | tf_op jit(solution)/shard_map/all_to_all | solution.py:80
  154.8 27.8 %reduce-scatter.7.cloned.1.call-start = ((), (), s32[]{:S(2)}) async-start(), calls=%async_computation.6 | async-start | bytes 163840 | tf_op jit(solution)/shard_map/reduce_scatter | solution.py:81
  162.1 0.7 copy-start.3
  162.8 211.0 %reduce-scatter.9.cloned.1.call-start = ((), (), s32[]{:S(2)}) async-start(), calls=%async_computation.7 | async-start | bytes 4718592 | tf_op jit(solution)/shard_map/reduce_scatter | solution.py:151
  183.5 102.1 %copy-start.4 = (f32[8,1024]{1,0:T(8,128)}, f32[8,1024]{1,0:T(8,128)S(1)}, u32[]{:S(2)}) copy-start(f32[8,1024]{1,0:T(8,128)S(1)} %get-tuple-element.7) | copy-start | bytes 98308
  232.0 31.7 %copy-start.5 = (f32[64,64]{0,1:T(8,128)}, f32[64,64]{0,1:T(8,128)S(1)}, u32[]{:S(2)}) copy-start(f32[64,64]{0,1:T(8,128)S(1)} %get-tuple-element.5) | copy-start | bytes 49156
  285.6 180.3 %reduce-scatter.11.cloned.1.call-start = ((), (), s32[]{:S(2)}) async-start(), calls=%async_computation.8 | async-start | bytes 4718592 | tf_op jit(solution)/shard_map/reduce_scatter | solution.py:159
Sparse Core Ops, SparseCore 0:
  51.2 66.8 reduce-scatter.4
  162.9 19.6 reduce-scatter.6
  285.7 88.0 reduce-scatter.8
  377.9 87.9 reduce-scatter.10
where the time goes:
time: 473 us; the launch traced here: 472 us
  waiting for transfers between devices  229 us (48%)
  blocking collectives  145 us (31%)
  matrix products  53.3 us (11%)
  other arithmetic  21.7 us (5%)
  between operations  14 us (3%)
  local copies, waits for them, and re-layouts  5.31 us (1%)
    reduce_scatter x1, waiting for transfers between devices, on_device(): lax.psum_scatter(grad_out_part, 'dp', scatter_dimension=0, tiled=True)  92.1 us
    reduce_scatter x1, waiting for transfers between devices, on_device(): lax.psum_scatter(lax.dot_general(tokens, act_grad, (((0,), (0,)), ((), ()...  85.4 us
    all_gather x1, blocking collectives, on_device(): every_row = lax.all_gather(normed, 'dp', axis=0, tiled=True)  35.3 us
    reduce_scatter x1, waiting for transfers between devices, on_device(): lax.psum_scatter(jnp.concatenate([gate_part, upper_part], axis=1), 'dp',...  32.8 us
    all_gather x1, blocking collectives, on_device(): lax.all_gather(teacher_normalized, 'dp', axis=0, tiled=True)  31.1 us
    all_gather x1, blocking collectives, on_device(): lax.all_gather(hidden, 'dp', axis=0, tiled=True)  31 us
    all_gather x1, blocking collectives, on_device(): lax.all_gather(student_normalized, 'dp', axis=0, tiled=True)  30.9 us
    reduce_scatter x1, waiting for transfers between devices, on_device(): lax.psum_scatter(per_doc, 'section', scatter_dimension=1, tiled=True)  17.8 us
  transfers between devices with their start and end apart: 5, of which 5 were waited for; matrix products, arithmetic and copies ran while one was open for 9% of the time, Pallas kernels for 0%

commit v1 on v0

--- a/solution.py
+++ b/solution.py
@@ -110,8 +110,17 @@
     norms = jnp.sqrt(jnp.sum(student_raw * student_raw, -1, keepdims=True) + 1e-06)
     student_normalized = student_raw / norms
     teacher_normalized = scaled / jnp.sqrt(teacher_total[:, None] + 1e-06)
+
+    def create_array(frame, ax_name):
+        panels = []
+        for _ in range(jax.lax.axis_size(ax_name)):
+            panels.append(frame)
+        back = jnp.stack(panels)
+        near = jax.lax.all_to_all(back, ax_name, split_axis=0, concat_axis=0)
+        return jnp.concatenate(near, axis=0)
+
     all_student_rows, every_teacher = (
-        lax.all_gather(student_normalized, "dp", axis=0, tiled=True),
+        create_array(student_normalized, "dp"),
         lax.all_gather(teacher_normalized, "dp", axis=0, tiled=True),
     )
     first_row = dp_index * local_docs

time: 473 us -> 456 us (0.964)
  blocking collectives: 145 us -> 114 us
  waiting for transfers between devices: 229 us -> 236 us
  starting transfers between devices: 3.54 us -> 9 us
    all_gather x1 -> x0, blocking collectives: 30.9 us -> none  [on_device(): lax.all_gather(student_normalized, 'dp', axis=0, tiled=True)]
    all_to_all x0 -> x1, waiting for transfers between devices: none -> 7.72 us  [create_array(): near = jax.lax.all_to_all(back, ax_name, split_axis=0, concat_axis=0)]
    all_to_all x0 -> x1, starting transfers between devices: none -> 5.29 us  [create_array(): near = jax.lax.all_to_all(back, ax_name, split_axis=0, concat_axis=0)]
  transfers between devices with their start and end apart: 5 -> 6, of which waited for: 5 -> 6; matrix products, arithmetic and copies ran while one was open for 9% -> 9% of each run, Pallas kernels for 0% -> 0%
where the time goes in v1:
time: 456 us; the launch traced here: 455 us
  waiting for transfers between devices  236 us (52%)
  blocking collectives  114 us (25%)
  matrix products  53.3 us (12%)
  other arithmetic  21.7 us (5%)
  between operations  14 us (3%)
  starting transfers between devices  9 us (2%)
  local copies, waits for them, and re-layouts  6.57 us (1%)
    reduce_scatter x1, waiting for transfers between devices, on_device(): lax.psum_scatter(grad_out_part, 'dp', scatter_dimension=0, tiled=True)  92.1 us
    reduce_scatter x1, waiting for transfers between devices, on_device(): lax.psum_scatter(lax.dot_general(tokens, act_grad, (((0,), (0,)), ((), ()...  84.1 us
    all_gather x1, blocking collectives, on_device(): every_row = lax.all_gather(normed, 'dp', axis=0, tiled=True)  35.3 us
    reduce_scatter x1, waiting for transfers between devices, on_device(): lax.psum_scatter(jnp.concatenate([gate_part, upper_part], axis=1), 'dp',...  32.8 us
    all_gather x1, blocking collectives, on_device(): lax.all_gather(teacher_normalized, 'dp', axis=0, tiled=True)  31.1 us
    all_gather x1, blocking collectives, on_device(): lax.all_gather(hidden, 'dp', axis=0, tiled=True)  31 us
    reduce_scatter x1, waiting for transfers between devices, on_device(): lax.psum_scatter(per_doc, 'section', scatter_dimension=1, tiled=True)  17.8 us
    psum x2, blocking collectives, on_device(): emb_sum, teacher_total = lax.psum((partial_emb, teacher_square), 'section')  16.9 us
  transfers between devices with their start and end apart: 6, of which 6 were waited for; matrix products, arithmetic and copies ran while one was open for 9% of the time, Pallas kernels for 0%

profile of v1, /device:TPU:0, one launch (start us, length us, event | category | flops | bytes accessed | tf_op | source)
XLA Modules:
  0.0 454.7 jit_solution(17839511810909865384)
XLA Ops:
  7.2 0.0 copy-start
  7.2 0.0 reduce-scatter.5.cloned.1.call-start
  7.2 1.1 multiply_reduce_fusion
  8.4 0.9 multiply_convert_fusion.5
  9.3 35.3 %all_gather.9 = bf16[64,4096]{1,0:T(8,128)(2,1)} all-gather(bf16[8,4096]{1,0:T(8,128)(2,1)S(1)} %multiply_convert_fusion.5), channel_id=1, replica_groups=mesh['section'=4,'dp'=8] {'dp'}, dimensions={0}, use_global_device_ids=true | all-gather | bytes 589824 | tf_op jit(solution)/shard_map/all_gather | solution.py:67
  44.6 2.6 fusion.12
  47.2 2.6 fusion.14
  49.8 1.3 pad_maximum_fusion
  51.0 0.0 reduce-scatter.5.cloned.1.call-update
  51.1 0.0 copy-start.7
  51.1 0.0 slice-start
  51.1 0.0 copy-start.6
  51.1 4.7 %convert_reduce_fusion = f32[8,512]{1,0:T(8,128)S(1)} fusion(bf16[8,512,1024]{2,1,0:T(8,128)(2,1)} %param.10), kind=kLoop, calls=%fused_computation.2 | loop fusion | flops 8384512 | bytes 8404992 | tf_op jit(solution)/shard_map/reduce_sum | solution.py:12
  55.8 0.0 slice-start.1
  55.8 5.7 %fusion.2 = f32[8,512]{1,0:T(8,128)S(1)} fusion(bf16[8,512,1024]{2,1,0:T(8,128)(2,1)} %param.10, f32[8,512]{1,0:T(8,128)S(1)} %broadcast_multiply_fusion), kind=kLoop, calls=%fused_computation.5 | loop fusion | flops 16773120 | bytes 8421376 | tf_op jit(solution)/shard_map/reduce_sum | solution.py:13
  61.6 0.7 fusion.29
  62.2 0.0 copy-done.6
  62.2 2.8 fusion.4
  65.1 0.0 copy-start.8
  65.1 1.2 fusion.32
  66.3 2.4 copy-done.1
  68.7 16.7 %fusion.8 = (f32[4096,1024]{1,0:T(8,128)}, bf16[4096,1024]{1,0:T(8,128)(2,1)}) fusion(bf16[4096,1024]{1,0:T(8,128)(2,1)S(1)} %bitcast.62, bf16[1024,1024]{1,0:T(8,128)(2,1)S(1)} %copy-done.8), kind=kOutput, calls=%fused_computation.11 | convolution fusion | flops 8636071936 | bytes 35651584 | tf_op jit(solution)/shard_map/dot_general | solution.py:94
  85.3 32.8 %reduce-scatter.5.cloned.1.call-done = f32[8,6144]{1,0:T(8,128)} async-done(((f32[64,6144]{1,0:T(8,128)}), f32[8,6144]{1,0:T(8,128)}) %reduce-scatter.5.cloned.1.call-update) | async-done | bytes 196624 | tf_op jit(solution)/shard_map/reduce_scatter | solution.py:71
  118.1 1.0 fusion.21
  119.1 31.0 %all_gather.10 = bf16[64,3072]{1,0:T(8,128)(2,1)S(1)} all-gather(bf16[8,3072]{1,0:T(8,128)(2,1)S(1)} %fusion.21), channel_id=1, replica_groups=mesh['section'=4,'dp'=8] {'dp'}, dimensions={0}, use_global_device_ids=true | all-gather | bytes 442368 | tf_op jit(solution)/shard_map/all_gather | solution.py:76
  150.1 1.3 convolution_bitcast_fusion
  151.4 3.4 all-to-all-start.1
  154.8 0.0 reduce-scatter.7.cloned.1.call-start
  154.9 4.6 %fusion.30 = f32[8,1,1024]{2,1,0:T(1,128)S(1)} fusion(bf16[8,512,1024]{2,1,0:T(8,128)(2,1)} %bitcast.61, bf16[8,512,1]{1,0,2:T(8,128)(2,1)S(1)} %get-tuple-element.13), kind=kOutput, calls=%fused_computation.61 | convolution fusion | flops 8388608 | bytes 8429568 | tf_op jit(solution)/shard_map/bs,bsf->bf/dot_general | solution.py:101
  159.4 0.7 convert_element_type.50
  160.1 0.7 dynamic_slice.17
  160.8 1.3 all-to-all-done.1
  162.1 0.7 copy-done.3
  162.7 0.0 reduce-scatter.7.cloned.1.call-update
  162.8 2.0 fusion.42
  164.8 17.8 %reduce-scatter.7.cloned.1.call-done = f32[8,1024]{1,0:T(8,128)} async-done(((f32[8,4096]{1,0:T(8,128)}), f32[8,1024]{1,0:T(8,128)}) %reduce-scatter.7.cloned.1.call-update) | async-done | bytes 32784 | tf_op jit(solution)/shard_map/reduce_scatter | solution.py:81
  182.6 0.9 multiply_reduce_fusion.2
  183.5 5.8 %psum.22 = f32[8]{0:T(128)S(1)} all-reduce(f32[8]{0:T(128)S(1)} %get-tuple-element.6), channel_id=1, replica_groups=mesh['section'=4,'dp'=8] {'section'}, use_global_device_ids=true, to_apply=%region_9.10 | all-reduce | flops 8 | bytes 64 | tf_op jit(solution)/shard_map/psum | solution.py:108
  189.3 0.1 multiply_divide_fusion
  189.3 31.1 %all_gather.11 = f32[64,1024]{1,0:T(8,128)S(1)} all-gather(f32[8,1024]{1,0:T(8,128)S(1)} %multiply_divide_fusion), channel_id=1, replica_groups=mesh['section'=4,'dp'=8] {'dp'}, dimensions={0}, use_global_device_ids=true | all-gather | bytes 294912 | tf_op jit(solution)/shard_map/all_gather | solution.py:124
  220.5 0.4 fusion.44
  220.9 11.1 %all-reduce = (f32[8,1024]{1,0:T(8,128)S(1)}, f32[64,64]{0,1:T(8,128)S(1)}) all-reduce(f32[8,1024]{1,0:T(8,128)S(1)} %fusion.42, f32[64,64]{0,1:T(8,128)S(1)} %fusion.44), channel_id=1, replica_groups=mesh['section'=4,'dp'=8] {'section'}, use_global_device_ids=true, to_apply=%region_2.3 | all-reduce | flops 12288 | bytes 98304 | tf_op jit(solution)/shard_map/psum | solution.py:108
  232.0 0.0 copy-start.5
  232.0 0.2 multiply_reduce_fusion.3
  232.2 0.1 broadcast_divide_fusion
  232.3 0.7 stack.2
  233.0 5.3 %all-to-all-start = ((f32[8,8,1024]{2,1,0:T(8,128)}), f32[8,8,1024]{2,1,0:T(8,128)S(1)}, u32[]{:S(2)}, u32[]{:S(2)}) async-start(f32[8,8,1024]{2,1,0:T(8,128)} %stack.2), calls=%async_computation | async-start | bytes 524288 | tf_op jit(solution)/shard_map/all_to_all | solution.py:119
  238.3 0.2 reduce-scatter.9.cloned.1.call-start
  238.6 0.5 log.17
  239.1 7.7 %all-to-all-done = f32[8,8,1024]{2,1,0:T(8,128)S(1)} async-done(((f32[8,8,1024]{2,1,0:T(8,128)}), f32[8,8,1024]{2,1,0:T(8,128)S(1)}, u32[]{:S(2)}, u32[]{:S(2)}) %all-to-all-start) | async-done | bytes 262176 | tf_op jit(solution)/shard_map/all_to_all | solution.py:119
  246.8 0.4 fusion.26
  247.2 1.4 subtract_subtract_fusion
  248.6 0.7 constant_dynamic-slice_fusion
  249.3 0.8 copy.22
  250.1 0.4 multiply_reduce_fusion.1
  250.5 0.1 divide_convert_fusion
  250.6 2.2 convolution_divide_fusion
  252.8 16.3 %fusion.18 = f32[1024,1024]{1,0:T(8,128)} fusion(bf16[8,512,1024]{2,1,0:T(8,128)(2,1)} %copy-done.1, f32[8,512,1024]{2,1,0:T(8,128)} %bitcast.64, f32[8,1024]{1,0:T(8,128)S(1)} %convolution_divide_fusion, f32[8,512]{1,0:T(8,128)} %get-tuple-element.12), kind=kOutput, calls=%fused_computation.24 | convolution fusion | flops 8602517504 | bytes 29409280 | tf_op jit(solution)/shard_map/dot_general | solution.py:161
  269.1 0.0 reduce-scatter.9.cloned.1.call-update
  269.2 0.0 reduce-scatter.11.cloned.1.call-start
  269.2 2.8 fusion.40
  272.0 0.0 reduce-scatter.11.cloned.1.call-update
  272.0 84.1 %reduce-scatter.9.cloned.1.call-done = f32[128,1024]{1,0:T(8,128)} async-done(((f32[1024,1024]{1,0:T(8,128)}), f32[128,1024]{1,0:T(8,128)}) %reduce-scatter.9.cloned.1.call-update) | async-done | bytes 524304 | tf_op jit(solution)/shard_map/reduce_scatter | solution.py:160
  356.1 92.1 %reduce-scatter.11.cloned.1.call-done = f32[128,1024]{1,0:T(8,128)} async-done(((f32[1024,1024]{1,0:T(8,128)}), f32[128,1024]{1,0:T(8,128)}) %reduce-scatter.11.cloned.1.call-update) | async-done | bytes 524304 | tf_op jit(solution)/shard_map/reduce_scatter | solution.py:168
  (22 shorter events, 0.1 us)
Async XLA Ops:
  7.2 142.9 %copy-start = (bf16[3072,512]{1,0:T(8,128)(2,1)S(1)}, bf16[3072,512]{1,0:T(8,128)(2,1)}, u32[]{:S(2)}) copy-start(bf16[3072,512]{1,0:T(8,128)(2,1)} %param.18) | copy-start | bytes 9437188
  7.2 110.9 %reduce-scatter.5.cloned.1.call-start = ((), (), s32[]{:S(2)}) async-start(), calls=%async_computation.6 | async-start | bytes 1769472 | tf_op jit(solution)/shard_map/reduce_scatter | solution.py:71
  51.1 10.5 %copy-start.7 = (s32[8]{0:T(128)S(1)}, s32[8]{0:T(128)}, u32[]{:S(2)}) copy-start(s32[8]{0:T(128)} %param.11) | copy-start | bytes 100
  51.1 11.2 %slice-start = ((s8[8388608]{0:T(1024)(128)(4,1)}), s8[4194304]{0:T(1024)(128)(4,1)S(1)}, s32[]{:S(2)}) async-start(s8[8388608]{0:T(1024)(128)(4,1)} %bitcast.59), calls=%async_computation.10 | async-start | bytes 8388608
  51.1 11.2 %copy-start.6 = (f32[1024]{0:T(1024)S(1)}, f32[1024]{0:T(1024)}, u32[]{:S(2)}) copy-start(f32[1024]{0:T(1024)} %param.12) | copy-start | bytes 12292
  55.8 6.4 %slice-start.1 = ((s8[8388608]{0:T(1024)(128)(4,1)}), s8[4194304]{0:T(1024)(128)(4,1)S(1)}, s32[]{:S(2)}) async-start(s8[8388608]{0:T(1024)(128)(4,1)} %bitcast.59), calls=%async_computation.11 | async-start | bytes 8388608
  65.1 3.6 copy-start.1
  65.1 3.6 copy-start.8
  85.3 74.1 %copy-start.2 = (bf16[8,4096]{1,0:T(8,128)(2,1)S(1)}, bf16[8,4096]{1,0:T(8,128)(2,1)}, u32[]{:S(2)}) copy-start(bf16[8,4096]{1,0:T(8,128)(2,1)} %param.15) | copy-start | bytes 196612
  151.4 10.7 %all-to-all-start.1 = ((f32[8,8,512]{2,1,0:T(8,128)}), f32[8,8,512]{2,1,0:T(8,128)S(1)}, u32[]{:S(2)}, u32[]{:S(2)}) async-start(f32[8,8,512]{2,1,0:T(8,128)} %convolution_bitcast_fusion), calls=%async_computation.2 | async-start | bytes 262144 | tf_op jit(solution)/shard_map/all_to_all | solution.py:80
  154.8 27.8 %reduce-scatter.7.cloned.1.call-start = ((), (), s32[]{:S(2)}) async-start(), calls=%async_computation.7 | async-start | bytes 163840 | tf_op jit(solution)/shard_map/reduce_scatter | solution.py:81
  162.1 0.7 copy-start.3
  183.5 85.7 %copy-start.4 = (f32[8,1024]{1,0:T(8,128)}, f32[8,1024]{1,0:T(8,128)S(1)}, u32[]{:S(2)}) copy-start(f32[8,1024]{1,0:T(8,128)S(1)} %get-tuple-element.7) | copy-start | bytes 98308
  232.0 15.3 %copy-start.5 = (f32[64,64]{0,1:T(8,128)}, f32[64,64]{0,1:T(8,128)S(1)}, u32[]{:S(2)}) copy-start(f32[64,64]{0,1:T(8,128)S(1)} %get-tuple-element.5) | copy-start | bytes 49156
  233.0 13.8 %all-to-all-start = ((f32[8,8,1024]{2,1,0:T(8,128)}), f32[8,8,1024]{2,1,0:T(8,128)S(1)}, u32[]{:S(2)}, u32[]{:S(2)}) async-start(f32[8,8,1024]{2,1,0:T(8,128)} %stack.2), calls=%async_computation | async-start | bytes 524288 | tf_op jit(solution)/shard_map/all_to_all | solution.py:119
  238.3 117.8 %reduce-scatter.9.cloned.1.call-start = ((), (), s32[]{:S(2)}) async-start(), calls=%async_computation.8 | async-start | bytes 4718592 | tf_op jit(solution)/shard_map/reduce_scatter | solution.py:160
  269.2 179.0 %reduce-scatter.11.cloned.1.call-start = ((), (), s32[]{:S(2)}) async-start(), calls=%async_computation.9 | async-start | bytes 4718592 | tf_op jit(solution)/shard_map/reduce_scatter | solution.py:168
Sparse Core Ops, SparseCore 0:
  51.2 66.8 reduce-scatter.4
  162.9 19.6 reduce-scatter.6
  269.3 86.7 reduce-scatter.8
  360.2 87.9 reduce-scatter.10
